TPU v7x, 512 devices: a whole 4x8x8 slice. The times are simulated.
512 devices in a mesh: band: 2 (over core), tmpl: 32 (over z, x), tm: 8 (over y).
Axes of the slice: x: 4, y: 8, z: 8, core: 2. Of those that a mesh axis runs over, the one named last changes fastest.
Arguments:
- strain_high: float32 [65536], P('tm'), may hold values from -6 to 6
- strain_mid: float32 [8192], P('tm'), may hold values from -6 to 6
- strain_low: float32 [1024], P('tm'), may hold values from -6 to 6
- filters_high: float32 [320, 1024], P('tmpl'), may hold values from -0.1875 to 0.1875
- filters_mid: float32 [320, 1024], P('tmpl'), may hold values from -0.1875 to 0.1875
- filters_low: float32 [320, 128], P('tmpl'), may hold values from -0.5 to 0.5
- recon_high: float32 [320, 2, 2048], P(None, None, 'tmpl'), may hold values from -0.3125 to 0.3125
- recon_mid: float32 [320, 2, 2048], P(None, None, 'tmpl'), may hold values from -0.3125 to 0.3125
- recon_low: float32 [320, 2, 2048], P(None, None, 'tmpl'), may hold values from -0.3125 to 0.3125
- basis_count: int32 [3], replicated, may hold values from 160 to 320
Outputs:
- snr: float32 [2, 2048, 65536], P('band', 'tmpl', 'tm')
Inputs may be any that keep to these rules, and one draw needn't show every extreme that they name: basis_count[b] says how many of the first 320 basis vectors band b uses.
All inputs are finite; a program needn't handle non-finite values.
Results may differ from a plain program's by a relative error of at most 0.000082.
Values sent between devices are 32-bit elements; how exact they have to be, the bound alone decides.
No kernel may reach another device: no remote copies, remote signals or barrier semaphores. Data moves between devices by JAX's collectives and lax.ppermute only.
A program may use at most 128 MiB of HBM per device.

v0:
```python
import math

import jax
import jax.numpy as jnp
from jax import lax
from jax.sharding import PartitionSpec as P

RATIO = 8
HALF_TAPS = 8


highest = lax.Precision.HIGHEST


def from_behind(value, axis, by):
    peers = lax.axis_size(axis)
    pairs = [(i, i + by) for i in range(peers) if 0 <= i + by < peers]
    return lax.ppermute(value, axis, pairs)


def extended_2(block, sides, width):
    for axis, dim in sides:
        count = lax.axis_size(axis)
        forward = [(i, i + 1) for i in range(count - 1)]
        backward = [(target, source) for source, target in forward]
        low = lax.ppermute(
            lax.slice_in_dim(block, block.shape[dim] - width, None, axis=dim), axis, forward
        )
        high = lax.ppermute(lax.slice_in_dim(block, 0, width, axis=dim), axis, backward)
        block = jnp.concatenate([low, block, high], axis=dim)
    return block


def interp_value(offset, half_taps):
    return jnp.sinc(offset) * (0.5 + 0.5 * jnp.cos(jnp.pi * offset / (half_taps + 1)))


def upsample_matrix(half_taps):
    block_len = 2 * half_taps
    inner_idx = lax.broadcasted_iota(jnp.int32, (2 * block_len, RATIO * block_len), 0)
    outer_idx = lax.broadcasted_iota(jnp.int32, (2 * block_len, RATIO * block_len), 1)
    lag_index = inner_idx - outer_idx // RATIO
    phase_frac = (outer_idx % RATIO).astype(jnp.float32) / RATIO
    kernel_val = interp_value(phase_frac - (lag_index - half_taps).astype(jnp.float32), half_taps)
    return jnp.where((lag_index >= 0) & (lag_index < block_len), kernel_val, 0.0)


def upsample(extended, half_taps):
    channels, ext_len = extended.shape
    block_len = 2 * half_taps
    block_count = ext_len // block_len - 1
    pieces = extended.reshape(channels, block_count + 1, block_len)
    window = jnp.concatenate([pieces[:, :-1], pieces[:, 1:]], axis=2)
    matrix = upsample_matrix(half_taps)
    upsampled = jnp.einsum(
        "cbi,im->cbm", window, matrix, precision=highest, preferred_element_type=jnp.float32
    )
    return upsampled.reshape(channels, block_count * RATIO * block_len)


def basis_filter(series, past_tail, filter_rows):
    row_count, tap_count = filter_rows.shape
    block_width = math.gcd(tap_count, 128)
    block_count = tap_count // block_width
    sample_count = series.shape[0]
    joined = jnp.concatenate([past_tail, series, jnp.zeros((1,), jnp.float32)])
    joined_len = joined.shape[0]
    frame_len = sample_count + tap_count - block_width
    tiled_copy = jnp.tile(joined, block_width)[: block_width * (joined_len - 1)].reshape(
        block_width, joined_len - 1
    )
    frames = tiled_copy[:, block_width - 1 : block_width - 1 + frame_len]
    mixed_rows = jnp.dot(
        filter_rows.reshape(row_count * block_count, block_width),
        frames,
        precision=highest,
        preferred_element_type=jnp.float32,
    )
    mixed_rows = mixed_rows.reshape(row_count, block_count, frame_len)
    result = jnp.zeros((row_count, sample_count), jnp.float32)
    for block_idx in range(block_count):
        offset = (block_count - 1 - block_idx) * block_width
        result = result + mixed_rows[:, block_idx, offset : offset + sample_count]
    return result


def keep_rows(series, first_row, row_limit):
    row_index = first_row + lax.broadcasted_iota(jnp.int32, (series.shape[0], 1), 0)
    return jnp.where(row_index < row_limit, series, 0.0)


def contract(weights, series):
    return lax.dot_general(
        weights,
        series,
        (((0,), (0,)), ((), ())),
        precision=highest,
        preferred_element_type=jnp.float32,
    )


def local(
    strain_high,
    strain_mid,
    strain_low,
    filters_high,
    filters_mid,
    filters_low,
    recon_high,
    recon_mid,
    recon_low,
    basis_count,
):
    band_index = lax.axis_index("band")
    tmpl_index = lax.axis_index("tmpl")
    tmpl_count = lax.axis_size("tmpl")
    rows_here = filters_high.shape[0]
    basis_total = rows_here * tmpl_count
    sample_count = strain_high.shape[0]
    mid_count = strain_mid.shape[0]
    low_count = strain_low.shape[0]
    tmpl_local = recon_high.shape[2]
    first_row = tmpl_index * rows_here
    taps_high = filters_high.shape[1]
    taps_mid = filters_mid.shape[1]
    taps_low = filters_low.shape[1]
    past_tails = from_behind(
        (
            strain_high[sample_count - (taps_high - 1) :],
            strain_mid[mid_count - (taps_mid - 1) :],
            strain_low[low_count - (taps_low - 1) :],
        ),
        "tm",
        1,
    )
    half_rows = rows_here // 2
    half_first = band_index * half_rows
    global_first = first_row + half_first

    def own_half(strain, tail, filters, limit):
        picked = lax.dynamic_slice_in_dim(filters, half_first, half_rows, 0)
        return keep_rows(basis_filter(strain, tail, picked), global_first, limit).reshape(-1)

    packed = jnp.concatenate(
        [
            own_half(strain_high, past_tails[0], filters_high, basis_count[0]),
            own_half(strain_mid, past_tails[1], filters_mid, basis_count[1]),
            own_half(strain_low, past_tails[2], filters_low, basis_count[2]),
        ]
    )
    gathered = lax.all_gather(packed[None, :], ("band", "tmpl"), axis=0, tiled=True)
    high_end = half_rows * sample_count
    mid_end = high_end + half_rows * mid_count
    high_rows_all = gathered[:, :high_end].reshape(basis_total, sample_count)
    mid_rows = gathered[:, high_end:mid_end].reshape(basis_total, mid_count)
    low_rows = gathered[:, mid_end : mid_end + half_rows * low_count].reshape(
        basis_total, low_count
    )

    def pick_part(recon):
        chosen = lax.dynamic_index_in_dim(recon, band_index, 1, keepdims=False)
        chosen = chosen.reshape(tmpl_count, 2, half_rows, tmpl_local)
        return jnp.transpose(chosen, (1, 0, 2, 3)).reshape(basis_total, tmpl_local)

    high_weights = pick_part(recon_high)
    mid_weights = pick_part(recon_mid)
    low_weights = pick_part(recon_low)
    low_snr = contract(low_weights, low_rows)
    low_ext = extended_2(low_snr, (("tm", 1),), HALF_TAPS)
    mid_snr = contract(mid_weights, mid_rows) + upsample(low_ext, HALF_TAPS)
    mid_ext = extended_2(mid_snr, (("tm", 1),), HALF_TAPS)
    full_part = contract(high_weights, high_rows_all) + upsample(mid_ext, HALF_TAPS)
    return full_part.reshape(1, tmpl_local, sample_count)


def solution(mesh):
    in_specs = (
        P("tm"),
        P("tm"),
        P("tm"),
        P("tmpl", None),
        P("tmpl", None),
        P("tmpl", None),
        P(None, None, "tmpl"),
        P(None, None, "tmpl"),
        P(None, None, "tmpl"),
        P(),
    )
    out_specs = P("band", "tmpl", "tm")
    return jax.shard_map(local, mesh=mesh, in_specs=in_specs, out_specs=out_specs, check_vma=False)
```

profile of v0, /device:TPU:24, one launch (start us, length us, event | category | flops | bytes accessed | tf_op | source)
XLA Modules:
  0.0 218.3 jit_solution(7356848308661320937)
XLA Ops:
  6.5 0.8 slice.142
  7.3 4.7 %collective-permute-start.2 = (f32[127]{0:T(128)S(1)}, f32[127]{0:T(128)S(1)}, u32[]{:S(2)}, u32[]{:S(2)}) collective-permute-start(f32[127]{0:T(128)S(1)} %slice.142), channel_id=1, source_target_pairs={{0,1},{1,2},{2,3},{3,4},{4,5},{5,6},{6,7},{8,9},{9,10},{10,11},{11... | collective-permute-start | bytes 1532 | tf_op jit(solution)/shard_map/ppermute | solution.py:18
  12.0 0.8 slice.130
  12.8 2.6 %collective-permute-start.1 = (f32[1023]{0:T(1024)S(1)}, f32[1023]{0:T(1024)S(1)}, u32[]{:S(2)}, u32[]{:S(2)}) collective-permute-start(f32[1023]{0:T(1024)S(1)} %slice.130), channel_id=1, source_target_pairs={{0,1},{1,2},{2,3},{3,4},{4,5},{5,6},{6,7},{8,9},{9,10},{10,11},{11... | collective-permute-start | bytes 12284 | tf_op jit(solution)/shard_map/ppermute | solution.py:18
  15.4 0.8 slice.118
  16.1 2.6 %collective-permute-start = (f32[1023]{0:T(1024)S(1)}, f32[1023]{0:T(1024)S(1)}, u32[]{:S(2)}, u32[]{:S(2)}) collective-permute-start(f32[1023]{0:T(1024)S(1)} %slice.118), channel_id=1, source_target_pairs={{0,1},{1,2},{2,3},{3,4},{4,5},{5,6},{6,7},{8,9},{9,10},{10,11},{11... | collective-permute-start | bytes 12284 | tf_op jit(solution)/shard_map/ppermute | solution.py:18
  18.7 1.4 fusion.81
  20.1 1.3 fusion.42
  21.5 0.9 dynamic-slice_bitcast_fusion
  22.4 0.7 fusion.44
  23.2 0.1 broadcast_in_dim.52
  23.4 0.7 pad_maximum_fusion.2
  24.2 0.3 reshape.113
  24.5 0.9 fusion.2
  25.5 0.8 concatenate.25
  26.4 0.2 copy.45
  26.6 0.5 reshape.112
  27.1 0.8 fusion.7
  27.9 0.1 slice_add_fusion.7
  28.2 0.4 broadcast_bitcast_fusion
  28.6 3.0 %copy.43 = f32[16,72,8,128]{3,1,2,0:T(8,128)} copy(f32[16,72,8,128]{3,2,1,0:T(8,128)S(1)} %broadcast_bitcast_fusion) | data formatting | bytes 9437184
  31.6 7.2 %reshape.111 = f32[128,9215]{1,0:T(8,128)} reshape(f32[1179520]{0:T(1024)} %bitcast.71) | data formatting | bytes 9436160 | tf_op jit(solution)/shard_map/reshape | solution.py:69
  38.8 5.1 %fusion.1 = f32[5,8,9088]{2,1,0:T(8,128)S(1)} fusion(f32[128,9215]{1,0:T(8,128)} %reshape.111, f32[1,5,8,128]{3,1,2,0:T(8,128)S(1)} %get-tuple-element.22), kind=kOutput, calls=%fused_computation.4 | convolution fusion | flops 558366720 | bytes 6127616 | tf_op jit(solution)/shard_map/dot_general | solution.py:73
  43.9 0.9 slice_add_fusion
  44.9 0.8 reshape.134
  46.0 96.5 %all-gather.4.cloned.1.call-done = f32[64,1,46720]{2,1,0:T(1,128)} async-done(((f32[1,1,46720]{2,1,0:T(1,128)}), f32[64,1,46720]{2,1,0:T(1,128)}) %all-gather.4.cloned.1.call-update) | async-done | bytes 11960336 | tf_op jit(solution)/shard_map/all_gather | solution.py:151
  142.5 9.6 %copy.60 = f32[64,1,46720]{2,0,1:T(8,128)} copy(f32[64,1,46720]{2,1,0:T(1,128)} %all-gather.4.cloned.1.call-done) | data formatting | bytes 23920640
  152.1 0.9 slice.180
  153.0 0.4 fusion.82
  153.5 4.6 %collective-permute-start.3 = (f32[64,8]{1,0:T(8,128)S(1)}, f32[64,8]{1,0:T(8,128)S(1)}, u32[]{:S(2)}, u32[]{:S(2)}) collective-permute-start(f32[64,8]{1,0:T(8,128)S(1)} %get-tuple-element.12), channel_id=1, source_target_pairs={{0,1},{1,2},{2,3},{3,4},{4,5},{5,6},{6,7},{8,9},{9,10},{10,11},{11... | collective-permute-start | bytes 6152 | tf_op jit(solution)/shard_map/ppermute | solution.py:26
  158.1 2.1 collective-permute-start.4
  160.5 1.4 slice.179
  161.9 0.3 reshape.118
  162.3 2.9 %collective-permute-done.4 = f32[64,8]{1,0:T(8,128)S(1)} collective-permute-done((f32[64,8]{1,0:T(8,128)S(1)}, f32[64,8]{1,0:T(8,128)S(1)}, u32[]{:S(2)}, u32[]{:S(2)}) %collective-permute-start.4) | collective-permute-done | bytes 2080 | tf_op jit(solution)/shard_map/ppermute | solution.py:29
  165.4 0.1 copy.38
  165.5 0.1 copy.39
  165.7 0.5 fusion.8
  166.2 1.0 convolution_add_fusion.1
  167.3 1.9 collective-permute-start.6
  169.2 5.1 %collective-permute-start.5 = (f32[64,8]{1,0:T(8,128)S(1)}, f32[64,8]{1,0:T(8,128)S(1)}, u32[]{:S(2)}, u32[]{:S(2)}) collective-permute-start(f32[64,8]{1,0:T(8,128)S(1)} %get-tuple-element.9), channel_id=1, source_target_pairs={{0,1},{1,2},{2,3},{3,4},{4,5},{5,6},{6,7},{8,9},{9,10},{10,11},{11... | collective-permute-start | bytes 6152 | tf_op jit(solution)/shard_map/ppermute | solution.py:26
  174.6 8.6 %slice.178 = f32[64,40960]{1,0:T(8,128)} slice(f32[64,46720]{1,0:T(8,128)} %bitcast.70), slice={[0:64], [0:40960]} | slice | bytes 20971520 | tf_op jit(solution)/shard_map/slice | solution.py:154
  183.2 11.2 %reshape.115 = f32[320,8192]{1,0:T(8,128)} reshape(f32[64,40960]{1,0:T(8,128)} %slice.178) | data formatting | bytes 20971520 | tf_op jit(solution)/shard_map/reshape | solution.py:154
  194.4 0.2 concatenate.30
  194.6 0.2 copy.34
  194.9 0.4 copy.40
  195.2 0.4 copy.41
  195.6 3.5 %fusion.3 = f32[64,64,128]{2,1,0:T(8,128)S(1)} fusion(f32[64,64,16]{1,2,0:T(8,128)S(1)} %copy.41, f32[64,64,16]{1,2,0:T(8,128)S(1)} %copy.40, s32[128]{0:T(128)S(1)} %get-tuple-element.26, s32[128]{0:T(128)S(1)} %get-tuple-element.27, s32[128]{0:T(128)S(1)} %get-tuple-element.25, s32[128]{0:T(128)S(1)} %get-tuple-element.28, ...), kind=kOutput, calls=%fused_computation.9 | convolution fusion | flops 201658368 | bytes 2623744 | tf_op jit(solution)/shard_map/cbi,im->cbm/dot_general | solution.py:55
  199.1 12.4 %fusion = f32[1,64,8192]{2,1,0:T(8,128)} fusion(f32[320,64]{1,0:T(8,128)S(1)} %reshape.110, f32[320,8192]{1,0:T(8,128)} %reshape.115, f32[8,8,64,128]{3,2,1,0:T(8,128)S(1)} %bitcast.72), kind=kOutput, calls=%fused_computation.2 | convolution fusion | flops 2013790208 | bytes 14761984 | tf_op jit(solution)/shard_map/dot_general | solution.py:93
  (50 shorter events, 1.6 us)
Async XLA Ops:
  6.5 167.8 %copy-start = (f32[320,2,64]{0,2,1:T(8,128)S(1)}, f32[320,2,64]{0,2,1:T(8,128)}, u32[]{:S(2)}) copy-start(f32[320,2,64]{0,2,1:T(8,128)} %param.17) | copy-start | bytes 491524
  6.5 21.5 %copy-start.3 = (f32[8192]{0:T(1024)S(1)}, f32[8192]{0:T(1024)}, u32[]{:S(2)}) copy-start(f32[8192]{0:T(1024)} %param.11) | copy-start | bytes 98308
  6.5 136.0 %all-gather.4.cloned.1.call-start = ((), (), s32[]{:S(2)}) async-start(), calls=%async_computation | async-start | bytes 12147200 | tf_op jit(solution)/shard_map/all_gather | solution.py:151
  7.3 16.1 %collective-permute-start.2 = (f32[127]{0:T(128)S(1)}, f32[127]{0:T(128)S(1)}, u32[]{:S(2)}, u32[]{:S(2)}) collective-permute-start(f32[127]{0:T(128)S(1)} %slice.142), channel_id=1, source_target_pairs={{0,1},{1,2},{2,3},{3,4},{4,5},{5,6},{6,7},{8,9},{9,10},{10,11},{11... | collective-permute-start | bytes 1532 | tf_op jit(solution)/shard_map/ppermute | solution.py:18
  12.8 12.7 %collective-permute-start.1 = (f32[1023]{0:T(1024)S(1)}, f32[1023]{0:T(1024)S(1)}, u32[]{:S(2)}, u32[]{:S(2)}) collective-permute-start(f32[1023]{0:T(1024)S(1)} %slice.130), channel_id=1, source_target_pairs={{0,1},{1,2},{2,3},{3,4},{4,5},{5,6},{6,7},{8,9},{9,10},{10,11},{11... | collective-permute-start | bytes 12284 | tf_op jit(solution)/shard_map/ppermute | solution.py:18
  16.1 11.9 %collective-permute-start = (f32[1023]{0:T(1024)S(1)}, f32[1023]{0:T(1024)S(1)}, u32[]{:S(2)}, u32[]{:S(2)}) collective-permute-start(f32[1023]{0:T(1024)S(1)} %slice.118), channel_id=1, source_target_pairs={{0,1},{1,2},{2,3},{3,4},{4,5},{5,6},{6,7},{8,9},{9,10},{10,11},{11... | collective-permute-start | bytes 12284 | tf_op jit(solution)/shard_map/ppermute | solution.py:18
  38.8 6.9 %copy-start.1 = (f32[320,2,64]{0,2,1:T(8,128)S(1)}, f32[320,2,64]{0,2,1:T(8,128)}, u32[]{:S(2)}) copy-start(f32[320,2,64]{0,2,1:T(8,128)} %param.19) | copy-start | bytes 491524
  38.8 6.9 %copy-start.2 = (f32[320,2,64]{0,2,1:T(8,128)S(1)}, f32[320,2,64]{0,2,1:T(8,128)}, u32[]{:S(2)}) copy-start(f32[320,2,64]{0,2,1:T(8,128)} %param.18) | copy-start | bytes 491524
  153.5 8.7 %collective-permute-start.3 = (f32[64,8]{1,0:T(8,128)S(1)}, f32[64,8]{1,0:T(8,128)S(1)}, u32[]{:S(2)}, u32[]{:S(2)}) collective-permute-start(f32[64,8]{1,0:T(8,128)S(1)} %get-tuple-element.12), channel_id=1, source_target_pairs={{0,1},{1,2},{2,3},{3,4},{4,5},{5,6},{6,7},{8,9},{9,10},{10,11},{11... | collective-permute-start | bytes 6152 | tf_op jit(solution)/shard_map/ppermute | solution.py:26
  158.1 7.0 %collective-permute-start.4 = (f32[64,8]{1,0:T(8,128)S(1)}, f32[64,8]{1,0:T(8,128)S(1)}, u32[]{:S(2)}, u32[]{:S(2)}) collective-permute-start(f32[64,8]{1,0:T(8,128)S(1)} %get-tuple-element.13), channel_id=1, source_target_pairs={{1,0},{2,1},{3,2},{4,3},{5,4},{6,5},{7,6},{9,8},{10,9},{11,10},{12... | collective-permute-start | bytes 6152 | tf_op jit(solution)/shard_map/ppermute | solution.py:29
  167.3 27.1 %collective-permute-start.6 = (f32[64,8]{1,0:T(8,128)S(1)}, f32[64,8]{1,0:T(8,128)S(1)}, u32[]{:S(2)}, u32[]{:S(2)}) collective-permute-start(f32[64,8]{1,0:T(8,128)S(1)} %get-tuple-element.8), channel_id=1, source_target_pairs={{1,0},{2,1},{3,2},{4,3},{5,4},{6,5},{7,6},{9,8},{10,9},{11,10},{12... | collective-permute-start | bytes 6152 | tf_op jit(solution)/shard_map/ppermute | solution.py:29
  169.2 25.2 %collective-permute-start.5 = (f32[64,8]{1,0:T(8,128)S(1)}, f32[64,8]{1,0:T(8,128)S(1)}, u32[]{:S(2)}, u32[]{:S(2)}) collective-permute-start(f32[64,8]{1,0:T(8,128)S(1)} %get-tuple-element.9), channel_id=1, source_target_pairs={{0,1},{1,2},{2,3},{3,4},{4,5},{5,6},{6,7},{8,9},{9,10},{10,11},{11... | collective-permute-start | bytes 6152 | tf_op jit(solution)/shard_map/ppermute | solution.py:26
Sparse Core Ops, SparseCore 0:
  45.8 96.6 all-gather.3
where the time goes:
time: 219 us; the launch traced here: 218 us
  waiting for transfers between devices  99.5 us (45%)
  local copies, waits for them, and re-layouts  52.9 us (24%)
  matrix products  24.7 us (11%)
  starting transfers between devices  23.6 us (11%)
  between operations  13.9 us (6%)
  other arithmetic  3.86 us (2%)
    all_gather x1, waiting for transfers between devices, local(): lax.all_gather(packed[None, :], ('band', 'tmpl'), axis=0, tiled=True)  96.5 us
    unnamed x21, local copies, waits for them, and re-layouts  16.1 us
    dot_general x3, matrix products, contract(): lax.dot_general(weights, series, (((0,), (0,)), ((), ())), precision=high...  13.8 us
    reshape x1, local copies, waits for them, and re-layouts, local(): high_rows_all = gathered[:, :high_end].reshape(basis_total, sample_count)  11.2 us
    ppermute x3, starting transfers between devices, from_behind(): return lax.ppermute(value, axis, pairs)  9.83 us
    ppermute x2, starting transfers between devices, extended_2(): lax.ppermute(lax.slice_in_dim(block, block.shape[dim] - width, None, axis...  9.74 us
    slice x1, local copies, waits for them, and re-layouts, local(): high_rows_all = gathered[:, :high_end].reshape(basis_total, sample_count)  8.63 us
    reshape x3, local copies, waits for them, and re-layouts, basis_filter(): jnp.tile(joined, block_width)[:block_width * (joined_len - 1)]  8.07 us
  transfers between devices with their start and end apart: 8, of which 2 were waited for; matrix products, arithmetic and copies ran while one was open for 15% of the time, Pallas kernels for 0%

commit v1 on v0

v1 whole, which is shorter than its diff:
```python
import functools

import jax
import jax.numpy as jnp
import numpy as np
from jax import lax
from jax.experimental import pallas as pl
from jax.experimental.pallas import tpu as pltpu
from jax.sharding import PartitionSpec as P

RATIO = 8
HALF_TAPS = 8
LANES = 128
ROWS = 8
BF16 = jnp.bfloat16
F32 = jnp.float32


def interp_blocks():
    phase = np.arange(RATIO)[:, None] / RATIO
    lag = np.arange(2 * HALF_TAPS)[None, :]
    v = phase - (lag - HALF_TAPS)
    g = np.sinc(v) * (0.5 + 0.5 * np.cos(np.pi * v / (HALF_TAPS + 1)))
    blocks = np.zeros((4, 256, 256), np.float64)
    for r in range(4):
        for n in range(256):
            for q in range(2 * HALF_TAPS):
                blocks[r, 32 * r + n // RATIO + q, n] = g[n % RATIO, q]
    return blocks


def split(x):
    hi = x.astype(BF16)
    lo = (x - hi.astype(F32)).astype(BF16)
    return hi, lo


def dot(a, b):
    return lax.dot_general(a, b, (((1,), (0,)), ((), ())), preferred_element_type=F32)


def dot3(a_hi, a_lo, b_hi, b_lo):
    left = jnp.concatenate([a_hi, a_lo, a_hi], axis=1)
    right = jnp.concatenate([b_hi, b_hi, b_lo], axis=0)
    return dot(left, right)


def lane_iota(rows):
    return lax.broadcasted_iota(jnp.int32, (rows, LANES), 1)


def pack_filters(idx_ref, high_ref, mid_ref, low_ref, out_ref):
    band, slot = idx_ref[0], idx_ref[1]
    rows = high_ref.shape[0]
    start = pl.multiple_of(slot * LANES, LANES)
    high = high_ref[:, pl.ds(start, LANES)]
    mid = mid_ref[:, pl.ds(start, LANES)]
    main = jnp.where(band == 0, high, mid)
    low = pltpu.roll(low_ref[...], (LANES - 16 * slot) % LANES, 1)
    lane = lane_iota(1)
    line = [jnp.zeros((1, LANES), F32) for _ in range(2)]
    for q in range(rows):
        at = 16 * (q % 8)
        moved = low[q : q + 1, :]
        if at:
            moved = pltpu.roll(moved, at, 1)
        line[q // 8] = jnp.where((lane >= at) & (lane < at + 16), moved, line[q // 8])
    for p in range(out_ref.shape[0]):
        out_ref[p, 0:rows, :] = main
        out_ref[p, rows : rows + 1, :] = line[0]
        out_ref[p, rows + 1 : rows + 2, :] = line[1]
        out_ref[p, rows + 2 :, :] = jnp.zeros((out_ref.shape[1] - rows - 2, LANES), F32)


def combine(idx_ref, got_ref, high_ref, mid_ref, low_ref, tail_ref, smid_ref, slow_ref, out_ref, f_ref, fl_ref):
    band = idx_ref[0]
    limit = jnp.where(band == 0, idx_ref[2], idx_ref[3])
    limit_low = idx_ref[4]
    parts = got_ref.shape[0]
    basis = high_ref.shape[1]
    rows = basis // parts
    for q in range(rows):
        f_ref[pl.ds(q, parts, stride=rows), :] = got_ref[:, q, :]
        low = got_ref[:, rows + q // 8, :]
        at = 16 * (q % 8)
        if at:
            low = pltpu.roll(low, LANES - at, 1)
        fl_ref[pl.ds(q, parts, stride=rows), :] = low
    column = lax.broadcasted_iota(jnp.int32, high_ref.shape, 1)
    weights = jnp.where(column < limit, jnp.where(band == 0, high_ref[...], mid_ref[...]), 0.0)
    weights_low = jnp.where(column < limit_low, low_ref[...], 0.0)
    h = dot3(*split(weights), *split(f_ref[...]))
    h_low = jnp.transpose(dot3(*split(weights_low), *split(fl_ref[...])))[0:16, :]
    half = h.shape[0] // 2
    lane = lane_iota(ROWS)
    mid = smid_ref[...]
    mid_turned = pltpu.roll(mid, 64, 1)
    for part in range(2):
        turned = h_low if part == 0 else pltpu.roll(h_low, 64, 1)
        one_a = jnp.where(lane < 64, turned[0:8, :], mid_turned)
        one_b = jnp.where(lane < 64, turned[8:16, :], mid)
        last_a = jnp.where(band == 0, tail_ref[...], one_a)
        last_b = jnp.where(band == 0, jnp.broadcast_to(slow_ref[...], (ROWS, LANES)), one_b)
        for slot in range(out_ref.shape[0] // 2):
            at = part * (out_ref.shape[0] // 2) + slot
            out_ref[at, 0:half, :] = h[part * half : (part + 1) * half, :]
            out_ref[at, half : half + 8, :] = last_a
            out_ref[at, half + 8 : half + 16, :] = last_b


class Toeplitz:
    def __init__(self, source, shift, hi_ref, lo_ref):
        self.source, self.shift, self.hi_ref, self.lo_ref = source, shift, hi_ref, lo_ref
        self.turned = {}
        self.lane = lane_iota(ROWS)
        self.sub = lax.broadcasted_iota(jnp.int32, (ROWS, LANES), 0)

    def turn(self, group, n):
        key = (group, n)
        if key not in self.turned:
            by = (ROWS * group + self.shift) % LANES
            self.turned[key] = pltpu.roll(self.source(n), by, 1, stride=1, stride_axis=0)
        return self.turned[key]

    def eight(self, group, n):
        by = ROWS * group + self.shift
        amount = self.sub + by
        value = jnp.where(self.lane >= amount, self.turn(group, n), self.turn(group, n - 1))
        if by + ROWS - 1 > LANES:
            value = jnp.where(self.lane >= amount - LANES, value, self.turn(group, n - 2))
        return value

    def build(self, n, column):
        for pair in range(LANES // 16):
            value = jnp.concatenate([self.eight(2 * pair, n), self.eight(2 * pair + 1, n)], axis=0)
            hi, lo = split(value)
            at = (pl.ds(16 * pair, 16), pl.ds(LANES * column, LANES))
            self.hi_ref[at] = hi
            self.lo_ref[at] = lo


def wide(hi_ref, lo_ref, start, width):
    def pair(ref):
        return [ref[:, start : start + width], ref[:, start - LANES : start - LANES + width]]

    return jnp.concatenate(pair(hi_ref) + pair(hi_ref) + pair(lo_ref), axis=0)


def filter_and_rebuild(
    idx_ref, got_ref, strain_ref, up_hi_ref, up_lo_ref, out_ref,
    xh_ref, ym_ref, yl_ref, th_hi, th_lo, tm_hi, tm_lo, tl_hi, tl_lo, hh_ref, hm_ref, sm_ref,
):
    slot = idx_ref[1]
    slots = got_ref.shape[0] // 2
    tmpl = out_ref.shape[0]
    lane = lane_iota(ROWS)

    def fetch(by):
        index = jnp.clip(slot + by, 0, slots - 1)
        keep = (slot + by >= 0) & (slot + by < slots)
        zero = jnp.zeros((ROWS, LANES), F32)
        tail = jnp.where(keep, got_ref[index, 64:72, :], zero)
        low = jnp.where(keep, got_ref[index, 72:80, :], zero)[0:1, :]
        first = got_ref[slots + index, 64:72, :]
        second = got_ref[slots + index, 72:80, :]
        mid = jnp.where(lane < 64, pltpu.roll(first, 64, 1), second)
        return tail, jnp.where(keep, mid, zero), low

    tail_1, mid_1, low_1 = fetch(-1)
    _, mid_2, low_2 = fetch(-2)
    _, mid_0, low_0 = fetch(0)
    _, mid_r, low_r = fetch(1)
    xh_ref[0:8, :] = tail_1
    xh_ref[8:72, :] = strain_ref[...]
    ym_ref[0:8, :] = mid_2
    ym_ref[8:16, :] = mid_1
    ym_ref[16:24, :] = mid_0
    ym_ref[24:32, :] = mid_r
    yl_ref[0:1, :] = low_2
    yl_ref[1:2, :] = low_1
    yl_ref[2:3, :] = low_0
    yl_ref[3:4, :] = low_r

    for ref, first in ((hh_ref, 0), (hm_ref, slots)):
        for i in range(slots):
            hi, lo = split(got_ref[first + i, 0:tmpl, :])
            c, at = i // 2, LANES * (i % 2)
            rows = slice(c * tmpl, (c + 1) * tmpl)
            ref[rows, at : at + LANES] = hi
            ref[rows, 256 + at : 256 + at + LANES] = lo
            ref[rows, 512 + at : 512 + at + LANES] = hi
    h_low = jnp.transpose(jnp.concatenate([got_ref[slots + i, 64:80, :] for i in range(slots)], axis=0))[0:tmpl, :]

    def rows_of(ref):
        return lambda n: jnp.broadcast_to(ref[n : n + 1, :], (ROWS, LANES))

    low_t = Toeplitz(rows_of(yl_ref), 9, tl_hi, tl_lo)
    low_t.build(2, 0)
    low_t.build(3, 1)
    part_low = dot3(*split(h_low), tl_hi[...], tl_lo[...])
    low_count = LANES
    z = lax.broadcasted_iota(jnp.int32, part_low.shape, 1) - 9 + slot * low_count
    part_low = jnp.where((z >= 0) & (z < slots * low_count), part_low, 0.0)
    low_hi, low_lo = split(part_low)

    mid_t = Toeplitz(rows_of(ym_ref), 8, tm_hi, tm_lo)
    for n in range(1, 17):
        mid_t.build(n + 7 + 1, n)
    for r in range(4):
        sm_ref[:, 256 * r : 256 * r + 256] = dot3(low_hi, low_lo, up_hi_ref[r], up_lo_ref[r])
    edge = dot3(low_hi[:, LANES:], low_lo[:, LANES:], up_hi_ref[0, 0:LANES, 0:LANES], up_lo_ref[0, 0:LANES, 0:LANES])
    for c in range(4):
        edge = edge + dot(hm_ref[c * tmpl : (c + 1) * tmpl, :], wide(tm_hi, tm_lo, 2048 - 256 * c, LANES))
    for m in range(-3, 4):
        first, last = max(0, -m), min(3, 3 - m)
        got = dot(hm_ref[first * tmpl : (last + 1) * tmpl, :], wide(tm_hi, tm_lo, 256 * m + 1024, 256))
        for c in range(first, last + 1):
            at = 256 * (m + c)
            sm_ref[:, at : at + 256] += got[(c - first) * tmpl : (c - first + 1) * tmpl, :]
    sm_ref[:, 1024:1152] = edge
    mid_count = 1024
    v = lax.broadcasted_iota(jnp.int32, sm_ref.shape, 1) - 8 + slot * mid_count
    part_mid = jnp.where((v >= 0) & (v < slots * mid_count), sm_ref[...], 0.0)
    mid_hi, mid_lo = split(part_mid)

    def stacked(x):
        return jnp.concatenate([x[:, LANES * g : LANES * g + 256] for g in range(8)], axis=0)

    stack_hi, stack_lo = stacked(mid_hi), stacked(mid_lo)
    for r in range(4):
        got = dot3(stack_hi, stack_lo, up_hi_ref[r], up_lo_ref[r])
        for g in range(8):
            at = 1024 * g + 256 * r
            out_ref[:, at : at + 256] = got[g * tmpl : (g + 1) * tmpl, :]
    high_t = Toeplitz(rows_of(xh_ref), 0, th_hi, th_lo)
    blocks = out_ref.shape[1] // 256
    for n in (1, 2, 3):
        high_t.build(n, n)
    for m in range(-3, blocks):
        high_t.build(2 * m + 8, 2 * m + 8) if 2 * m + 8 > 3 else None
        high_t.build(2 * m + 9, 2 * m + 9) if 2 * m + 9 > 3 else None
        first, last = max(0, -m), min(3, blocks - 1 - m)
        got = dot(hh_ref[first * tmpl : (last + 1) * tmpl, :], wide(th_hi, th_lo, 256 * m + 1024, 256))
        for c in range(first, last + 1):
            at = 256 * (m + c)
            out_ref[:, at : at + 256] += got[(c - first) * tmpl : (c - first + 1) * tmpl, :]


VMEM = pl.BlockSpec(memory_space=pltpu.VMEM)
SMEM = pl.BlockSpec(memory_space=pltpu.SMEM)


def call_pack(idx, high, mid, low, parts, **kw):
    return pl.pallas_call(
        pack_filters,
        out_shape=jax.ShapeDtypeStruct((parts, 16, LANES), F32),
        in_specs=[SMEM] + [VMEM] * 3,
        out_specs=VMEM,
        name="pack_filters",
        **kw,
    )(idx, high, mid, low)


def call_combine(idx, got, high, mid, low, tail, smid, slow, peers, **kw):
    basis = high.shape[1]
    return pl.pallas_call(
        combine,
        out_shape=jax.ShapeDtypeStruct((peers, 80, LANES), F32),
        in_specs=[SMEM] + [VMEM] * 7,
        out_specs=VMEM,
        scratch_shapes=[pltpu.VMEM((basis, LANES), F32)] * 2,
        name="combine",
        **kw,
    )(idx, got, high, mid, low, tail, smid, slow)


def call_filter(idx, got, strain, up_hi, up_lo, tmpl, count, **kw):
    return pl.pallas_call(
        filter_and_rebuild,
        out_shape=jax.ShapeDtypeStruct((tmpl, count), F32),
        in_specs=[SMEM] + [VMEM] * 4,
        out_specs=VMEM,
        scratch_shapes=[
            pltpu.VMEM((72, LANES), F32),
            pltpu.VMEM((32, LANES), F32),
            pltpu.VMEM((8, LANES), F32),
            pltpu.VMEM((LANES, 9216), BF16),
            pltpu.VMEM((LANES, 9216), BF16),
            pltpu.VMEM((LANES, 2304), BF16),
            pltpu.VMEM((LANES, 2304), BF16),
            pltpu.VMEM((LANES, 256), BF16),
            pltpu.VMEM((LANES, 256), BF16),
            pltpu.VMEM((4 * tmpl, 768), BF16),
            pltpu.VMEM((4 * tmpl, 768), BF16),
            pltpu.VMEM((tmpl, 1152), F32),
        ],
        name="filter_and_rebuild",
        **kw,
    )(idx, got, strain, up_hi, up_lo)


def interp_halves():
    exact = jnp.asarray(interp_blocks().astype(np.float32))
    return split(exact)


def local(
    strain_high, strain_mid, strain_low,
    filters_high, filters_mid, filters_low,
    recon_high, recon_mid, recon_low, basis_count,
):
    band = lax.axis_index("band").astype(jnp.int32)
    slot = lax.axis_index("tm").astype(jnp.int32)
    tmpl_count = lax.axis_size("tmpl")
    peers = lax.axis_size("band") * lax.axis_size("tm")
    idx = jnp.concatenate([jnp.stack([band, slot]), basis_count, jnp.zeros((3,), jnp.int32)])
    packed = call_pack(idx, filters_high, filters_mid, filters_low, tmpl_count)
    got = lax.all_to_all(packed, "tmpl", 0, 0, tiled=True)

    def turned(recon):
        basis, parts, count = recon.shape
        return jnp.transpose(recon, (1, 2, 0)).reshape(parts * count, basis)

    rows = strain_high.reshape(-1, LANES)
    sent = call_combine(
        idx, got, turned(recon_high), turned(recon_mid), turned(recon_low),
        rows[-8:], strain_mid.reshape(-1, LANES), strain_low.reshape(1, LANES), peers,
    )
    here = lax.all_to_all(sent, ("band", "tm"), 0, 0, tiled=True)
    up_hi, up_lo = interp_halves()
    out = call_filter(idx, here, rows, up_hi, up_lo, recon_high.shape[2], strain_high.shape[0])
    return out[None]


def solution(mesh):
    in_specs = (
        P("tm"), P("tm"), P("tm"),
        P("tmpl", None), P("tmpl", None), P("tmpl", None),
        P(None, None, "tmpl"), P(None, None, "tmpl"), P(None, None, "tmpl"),
        P(),
    )
    out_specs = P("band", "tmpl", "tm")
    return jax.shard_map(local, mesh=mesh, in_specs=in_specs, out_specs=out_specs, check_vma=False)
```

time: 219 us -> 68.8 us (0.31)
  the two profiles are of different devices: /device:TPU:24 before, /device:TPU:1 now
where the time goes in v1:
time: 68.8 us; the launch traced here: 68.4 us
  blocking collectives  28.6 us (42%)
  starting transfers between devices  13.7 us (20%)
  Pallas kernels  12.9 us (19%)
  waiting for transfers between devices  10 us (15%)
  local copies, waits for them, and re-layouts  1.97 us (3%)
  other arithmetic  1.25 us (2%)
    all_to_all x1, blocking collectives, local(): here = lax.all_to_all(sent, ('band', 'tm'), 0, 0, tiled=True)  28.6 us
    all_to_all x1, starting transfers between devices, local(): got = lax.all_to_all(packed, 'tmpl', 0, 0, tiled=True)  13.7 us
    all_to_all x1, waiting for transfers between devices, local(): got = lax.all_to_all(packed, 'tmpl', 0, 0, tiled=True)  10 us
    pallas_call x1, Pallas kernels, call_filter(): pl.pallas_call(filter_and_rebuild, out_shape=jax.ShapeDtypeStruct((tmpl,...  8.48 us
    pallas_call x1, Pallas kernels, call_combine(): pl.pallas_call(combine, out_shape=jax.ShapeDtypeStruct((peers, 80, LANES)...  2.63 us
    pallas_call x1, Pallas kernels, call_pack(): pl.pallas_call(pack_filters, out_shape=jax.ShapeDtypeStruct((parts, 16, L...  1.75 us
  transfers between devices with their start and end apart: 1, of which 1 were waited for; matrix products, arithmetic and copies ran while one was open for 2% of the time, Pallas kernels for 0%

profile of v1, /device:TPU:1, one launch (start us, length us, event | category | flops | bytes accessed | tf_op | source)
XLA Modules:
  0.0 68.4 jit_solution(18443707582840341212)
XLA Ops:
  0.0 1.2 %pad_add_fusion.idx_ref = s32[8]{0:T(128)} fusion(s32[3]{0:T(128)S(1)} %broadcast.3, s32[3]{0:T(128)} %param.20, s32[1]{0:T(128)} %bitcast.1, s32[1]{0:T(128)} %bitcast), kind=kLoop, calls=%fused_computation.1 | loop fusion | flops 24 | bytes 64 | tf_op jit(solution)/shard_map/concatenate | solution.py:316
  1.3 1.8 %pack_filters.1 = f32[32,16,128]{2,1,0:T(8,128)} custom-call(s32[8]{0:T(128)} %pad_add_fusion.idx_ref, f32[10,1024]{1,0:T(8,128)} %high_ref.1, f32[10,1024]{1,0:T(8,128)} %mid_ref.1, f32[10,128]{1,0:T(8,128)} %low_ref.1), custom_call_target="tpu_custom_call" | custom-call | tf_op jit(solution)/shard_map/pack_filters/pallas_call | solution.py:254
  3.0 13.7 %all-to-all-start = ((f32[32,16,128]{2,1,0:T(8,128)}), f32[32,16,128]{2,1,0:T(8,128)S(1)}, u32[]{:S(2)}, u32[]{:S(2)}) async-start(f32[32,16,128]{2,1,0:T(8,128)} %pack_filters.1), calls=%async_computation | async-start | bytes 524288 | tf_op jit(solution)/shard_map/all_to_all | solution.py:318
  16.7 1.3 %slice_bitcast_fusion.tail_ref = f32[8,128]{1,0:T(8,128)} fusion(f32[8192]{0:T(1024)} %param.11), kind=kLoop, calls=%fused_computation | loop fusion | bytes 8192 | tf_op jit(solution)/shard_map/slice | solution.py:327
  18.0 10.0 %all-to-all-done.got_ref = f32[32,16,128]{2,1,0:T(8,128)S(1)} async-done(((f32[32,16,128]{2,1,0:T(8,128)}), f32[32,16,128]{2,1,0:T(8,128)S(1)}, u32[]{:S(2)}, u32[]{:S(2)}) %all-to-all-start) | async-done | bytes 262176 | tf_op jit(solution)/shard_map/all_to_all | solution.py:318
  28.0 0.0 copy-start
  28.0 0.7 %copy-done = f32[32,16,128]{2,1,0:T(8,128)} copy-done((f32[32,16,128]{2,1,0:T(8,128)}, f32[32,16,128]{2,1,0:T(8,128)S(1)}, u32[]{:S(2)}) %copy-start) | copy-done | bytes 262168
  28.7 2.6 %combine.1 = f32[16,80,128]{2,1,0:T(8,128)} custom-call(s32[8]{0:T(128)} %pad_add_fusion.idx_ref, f32[32,16,128]{2,1,0:T(8,128)} %copy-done, f32[128,320]{1,0:T(8,128)} %bitcast.17, f32[128,320]{1,0:T(8,128)} %bitcast.18, f32[128,320]{1,0:T(8,128)} %bitcast.19, f32[8,128]{1,0:T(8,128)} %slice_bitcast_fusion.tail_ref, f32[8,128]{1,0:T(8,128)} %bitcast.21, ...), custom_call_target="tpu_custom_call" | custom-call | tf_op jit(solution)/shard_map/combine/pallas_call | solution.py:266
  31.3 28.6 %all_to_all.10.got_ref = f32[16,80,128]{2,1,0:T(8,128)} all-to-all(f32[16,80,128]{2,1,0:T(8,128)} %combine.1), channel_id=1, replica_groups=mesh['band'=2,'tmpl'=32,'tm'=8] {'band','tm'}, dimensions={0} | all-to-all | bytes 1310720 | tf_op jit(solution)/shard_map/all_to_all | solution.py:329
  60.0 8.5 %filter_and_rebuild.1 = f32[64,8192]{1,0:T(8,128)} custom-call(s32[8]{0:T(128)} %pad_add_fusion.idx_ref, f32[16,80,128]{2,1,0:T(8,128)} %all_to_all.10.got_ref, f32[64,128]{1,0:T(8,128)} %bitcast.20, bf16[4,256,256]{2,1,0:T(8,128)(2,1)} %constant.18.up_hi_ref, bf16[4,256,256]{2,1,0:T(8,128)(2,1)} %constant.21.up_lo_ref), custom_call_target="tpu_custom_call" | custom-call | tf_op jit(solution)/shard_map/filter_and_rebuild/pallas_call | solution.py:278
  (1 shorter events, 0.0 us)
Async XLA Ops:
  3.0 25.0 %all-to-all-start = ((f32[32,16,128]{2,1,0:T(8,128)}), f32[32,16,128]{2,1,0:T(8,128)S(1)}, u32[]{:S(2)}, u32[]{:S(2)}) async-start(f32[32,16,128]{2,1,0:T(8,128)} %pack_filters.1), calls=%async_computation | async-start | bytes 524288 | tf_op jit(solution)/shard_map/all_to_all | solution.py:318
  28.0 0.7 %copy-start = (f32[32,16,128]{2,1,0:T(8,128)}, f32[32,16,128]{2,1,0:T(8,128)S(1)}, u32[]{:S(2)}) copy-start(f32[32,16,128]{2,1,0:T(8,128)S(1)} %all-to-all-done.got_ref) | copy-start | bytes 786436

commit v2 on v1

--- a/solution.py
+++ b/solution.py
@@ -45,12 +45,30 @@
     return dot(left, right)
 
 
+def rebuild(hi, lo, up_hi_ref, up_lo_ref, r):
+    if r == 3:
+        return dot3(hi, lo, up_hi_ref[r], up_lo_ref[r])
+    first_hi, first_lo = hi[:, :LANES], lo[:, :LANES]
+    return dot3(first_hi, first_lo, up_hi_ref[r, :LANES, :], up_lo_ref[r, :LANES, :])
+
+
 def lane_iota(rows):
     return lax.broadcasted_iota(jnp.int32, (rows, LANES), 1)
 
 
-def pack_filters(idx_ref, high_ref, mid_ref, low_ref, out_ref):
-    band, slot = idx_ref[0], idx_ref[1]
+def pack_filters(
+    place, count_ref, high_ref, mid_ref, low_ref, rhigh_ref, rmid_ref, rlow_ref, shigh_ref, smid_ref, slow_ref,
+    out_ref, w_hi_ref, w_lo_ref, l_hi_ref, l_lo_ref, strain_ref,
+):
+    band, slot = place()
+    strain_ref[0:64, :] = shigh_ref[...]
+    strain_ref[64:72, :] = smid_ref[...]
+    strain_ref[72:80, :] = jnp.broadcast_to(slow_ref[...], (ROWS, LANES))
+    column = lax.broadcasted_iota(jnp.int32, rhigh_ref.shape, 1)
+    limit = jnp.where(band == 0, count_ref[0], count_ref[1])
+    weights = jnp.where(column < limit, jnp.where(band == 0, rhigh_ref[...], rmid_ref[...]), 0.0)
+    w_hi_ref[...], w_lo_ref[...] = split(weights)
+    l_hi_ref[...], l_lo_ref[...] = split(jnp.where(column < count_ref[2], rlow_ref[...], 0.0))
     rows = high_ref.shape[0]
     start = pl.multiple_of(slot * LANES, LANES)
     high = high_ref[:, pl.ds(start, LANES)]
@@ -72,12 +90,10 @@
         out_ref[p, rows + 2 :, :] = jnp.zeros((out_ref.shape[1] - rows - 2, LANES), F32)
 
 
-def combine(idx_ref, got_ref, high_ref, mid_ref, low_ref, tail_ref, smid_ref, slow_ref, out_ref, f_ref, fl_ref):
-    band = idx_ref[0]
-    limit = jnp.where(band == 0, idx_ref[2], idx_ref[3])
-    limit_low = idx_ref[4]
+def combine(place, got_ref, w_hi_ref, w_lo_ref, l_hi_ref, l_lo_ref, strain_ref, out_ref, f_ref, fl_ref):
+    band, _ = place()
     parts = got_ref.shape[0]
-    basis = high_ref.shape[1]
+    basis = w_hi_ref.shape[1]
     rows = basis // parts
     for q in range(rows):
         f_ref[pl.ds(q, parts, stride=rows), :] = got_ref[:, q, :]
@@ -86,21 +102,18 @@
         if at:
             low = pltpu.roll(low, LANES - at, 1)
         fl_ref[pl.ds(q, parts, stride=rows), :] = low
-    column = lax.broadcasted_iota(jnp.int32, high_ref.shape, 1)
-    weights = jnp.where(column < limit, jnp.where(band == 0, high_ref[...], mid_ref[...]), 0.0)
-    weights_low = jnp.where(column < limit_low, low_ref[...], 0.0)
-    h = dot3(*split(weights), *split(f_ref[...]))
-    h_low = jnp.transpose(dot3(*split(weights_low), *split(fl_ref[...])))[0:16, :]
+    h = dot3(w_hi_ref[...], w_lo_ref[...], *split(f_ref[...]))
+    h_low = jnp.transpose(dot3(l_hi_ref[...], l_lo_ref[...], *split(fl_ref[...])))[0:16, :]
     half = h.shape[0] // 2
     lane = lane_iota(ROWS)
-    mid = smid_ref[...]
+    mid = strain_ref[64:72, :]
     mid_turned = pltpu.roll(mid, 64, 1)
     for part in range(2):
         turned = h_low if part == 0 else pltpu.roll(h_low, 64, 1)
         one_a = jnp.where(lane < 64, turned[0:8, :], mid_turned)
         one_b = jnp.where(lane < 64, turned[8:16, :], mid)
-        last_a = jnp.where(band == 0, tail_ref[...], one_a)
-        last_b = jnp.where(band == 0, jnp.broadcast_to(slow_ref[...], (ROWS, LANES)), one_b)
+        last_a = jnp.where(band == 0, strain_ref[56:64, :], one_a)
+        last_b = jnp.where(band == 0, strain_ref[72:80, :], one_b)
         for slot in range(out_ref.shape[0] // 2):
             at = part * (out_ref.shape[0] // 2) + slot
             out_ref[at, 0:half, :] = h[part * half : (part + 1) * half, :]
@@ -147,10 +160,10 @@
 
 
 def filter_and_rebuild(
-    idx_ref, got_ref, strain_ref, up_hi_ref, up_lo_ref, out_ref,
-    xh_ref, ym_ref, yl_ref, th_hi, th_lo, tm_hi, tm_lo, tl_hi, tl_lo, hh_ref, hm_ref, sm_ref,
+    place, got_ref, strain_ref, up_hi_ref, up_lo_ref, result_ref,
+    out_ref, sem_ref, xh_ref, ym_ref, yl_ref, th_hi, th_lo, tm_hi, tm_lo, tl_hi, tl_lo, hh_ref, hm_ref, sm_ref,
 ):
-    slot = idx_ref[1]
+    _, slot = place()
     slots = got_ref.shape[0] // 2
     tmpl = out_ref.shape[0]
     lane = lane_iota(ROWS)
@@ -171,7 +184,7 @@
     _, mid_0, low_0 = fetch(0)
     _, mid_r, low_r = fetch(1)
     xh_ref[0:8, :] = tail_1
-    xh_ref[8:72, :] = strain_ref[...]
+    xh_ref[8:72, :] = strain_ref[0:64, :]
     ym_ref[0:8, :] = mid_2
     ym_ref[8:16, :] = mid_1
     ym_ref[16:24, :] = mid_0
@@ -207,7 +220,7 @@
     for n in range(1, 17):
         mid_t.build(n + 7 + 1, n)
     for r in range(4):
-        sm_ref[:, 256 * r : 256 * r + 256] = dot3(low_hi, low_lo, up_hi_ref[r], up_lo_ref[r])
+        sm_ref[:, 256 * r : 256 * r + 256] = rebuild(low_hi, low_lo, up_hi_ref, up_lo_ref, r)
     edge = dot3(low_hi[:, LANES:], low_lo[:, LANES:], up_hi_ref[0, 0:LANES, 0:LANES], up_lo_ref[0, 0:LANES, 0:LANES])
     for c in range(4):
         edge = edge + dot(hm_ref[c * tmpl : (c + 1) * tmpl, :], wide(tm_hi, tm_lo, 2048 - 256 * c, LANES))
@@ -228,12 +241,18 @@
 
     stack_hi, stack_lo = stacked(mid_hi), stacked(mid_lo)
     for r in range(4):
-        got = dot3(stack_hi, stack_lo, up_hi_ref[r], up_lo_ref[r])
+        got = rebuild(stack_hi, stack_lo, up_hi_ref, up_lo_ref, r)
         for g in range(8):
             at = 1024 * g + 256 * r
             out_ref[:, at : at + 256] = got[g * tmpl : (g + 1) * tmpl, :]
     high_t = Toeplitz(rows_of(xh_ref), 0, th_hi, th_lo)
     blocks = out_ref.shape[1] // 256
+    copies = []
+
+    def chunk(k):
+        where = (slice(None), pl.ds(1024 * k, 1024))
+        return pltpu.make_async_copy(out_ref.at[where], result_ref.at[where], sem_ref.at[k])
+
     for n in (1, 2, 3):
         high_t.build(n, n)
     for m in range(-3, blocks):
@@ -244,43 +263,60 @@
         for c in range(first, last + 1):
             at = 256 * (m + c)
             out_ref[:, at : at + 256] += got[(c - first) * tmpl : (c - first + 1) * tmpl, :]
+        if m % 4 == 3 and m >= 0:
+            done = chunk(m // 4)
+            done.start()
+            copies.append(done)
+    for done in copies:
+        done.wait()
 
 
 VMEM = pl.BlockSpec(memory_space=pltpu.VMEM)
 SMEM = pl.BlockSpec(memory_space=pltpu.SMEM)
-
-
-def call_pack(idx, high, mid, low, parts, **kw):
+ANY = pl.BlockSpec(memory_space=pl.ANY)
+
+
+def near(x):
+    return pltpu.with_memory_space_constraint(x, pltpu.VMEM)
+
+
+def place():
+    return lax.axis_index("band").astype(jnp.int32), lax.axis_index("tm").astype(jnp.int32)
+
+
+def call_pack(count, filters, recons, strains, parts, place=place):
+    wide, basis = recons[0].shape
+    half = pltpu.VMEM((wide, basis), BF16)
     return pl.pallas_call(
-        pack_filters,
-        out_shape=jax.ShapeDtypeStruct((parts, 16, LANES), F32),
-        in_specs=[SMEM] + [VMEM] * 3,
-        out_specs=VMEM,
+        functools.partial(pack_filters, place),
+        out_shape=(pltpu.VMEM((parts, 16, LANES), F32), half, half, half, half, pltpu.VMEM((80, LANES), F32)),
+        in_specs=[SMEM] + [VMEM] * 9,
+        out_specs=(VMEM,) * 6,
         name="pack_filters",
-        **kw,
-    )(idx, high, mid, low)
-
-
-def call_combine(idx, got, high, mid, low, tail, smid, slow, peers, **kw):
-    basis = high.shape[1]
+    )(count, *filters, *recons, *strains)
+
+
+def call_combine(got, weights, strain, peers, place=place):
+    basis = weights[0].shape[1]
     return pl.pallas_call(
-        combine,
-        out_shape=jax.ShapeDtypeStruct((peers, 80, LANES), F32),
-        in_specs=[SMEM] + [VMEM] * 7,
+        functools.partial(combine, place),
+        out_shape=pltpu.VMEM((peers, 80, LANES), F32),
+        in_specs=[VMEM] * 6,
         out_specs=VMEM,
         scratch_shapes=[pltpu.VMEM((basis, LANES), F32)] * 2,
         name="combine",
-        **kw,
-    )(idx, got, high, mid, low, tail, smid, slow)
-
-
-def call_filter(idx, got, strain, up_hi, up_lo, tmpl, count, **kw):
+    )(*[near(x) for x in (got, *weights, strain)])
+
+
+def call_filter(got, strain, up_hi, up_lo, tmpl, count, place=place):
     return pl.pallas_call(
-        filter_and_rebuild,
+        functools.partial(filter_and_rebuild, place),
         out_shape=jax.ShapeDtypeStruct((tmpl, count), F32),
-        in_specs=[SMEM] + [VMEM] * 4,
-        out_specs=VMEM,
+        in_specs=[VMEM] * 4,
+        out_specs=ANY,
         scratch_shapes=[
+            pltpu.VMEM((tmpl, count), F32),
+            pltpu.SemaphoreType.DMA((count // 1024,)),
             pltpu.VMEM((72, LANES), F32),
             pltpu.VMEM((32, LANES), F32),
             pltpu.VMEM((8, LANES), F32),
@@ -295,8 +331,7 @@
             pltpu.VMEM((tmpl, 1152), F32),
         ],
         name="filter_and_rebuild",
-        **kw,
-    )(idx, got, strain, up_hi, up_lo)
+    )(*[near(x) for x in (got, strain, up_hi, up_lo)])
 
 
 def interp_halves():
@@ -309,26 +344,25 @@
     filters_high, filters_mid, filters_low,
     recon_high, recon_mid, recon_low, basis_count,
 ):
-    band = lax.axis_index("band").astype(jnp.int32)
-    slot = lax.axis_index("tm").astype(jnp.int32)
     tmpl_count = lax.axis_size("tmpl")
     peers = lax.axis_size("band") * lax.axis_size("tm")
-    idx = jnp.concatenate([jnp.stack([band, slot]), basis_count, jnp.zeros((3,), jnp.int32)])
-    packed = call_pack(idx, filters_high, filters_mid, filters_low, tmpl_count)
-    got = lax.all_to_all(packed, "tmpl", 0, 0, tiled=True)
 
     def turned(recon):
         basis, parts, count = recon.shape
         return jnp.transpose(recon, (1, 2, 0)).reshape(parts * count, basis)
 
-    rows = strain_high.reshape(-1, LANES)
-    sent = call_combine(
-        idx, got, turned(recon_high), turned(recon_mid), turned(recon_low),
-        rows[-8:], strain_mid.reshape(-1, LANES), strain_low.reshape(1, LANES), peers,
+    packed, *weights, strain = call_pack(
+        basis_count,
+        (filters_high, filters_mid, filters_low),
+        (turned(recon_high), turned(recon_mid), turned(recon_low)),
+        (strain_high.reshape(-1, LANES), strain_mid.reshape(-1, LANES), strain_low.reshape(1, LANES)),
+        tmpl_count,
     )
+    got = lax.all_to_all(packed, "tmpl", 0, 0, tiled=True)
+    sent = call_combine(got, weights, strain, peers)
     here = lax.all_to_all(sent, ("band", "tm"), 0, 0, tiled=True)
     up_hi, up_lo = interp_halves()
-    out = call_filter(idx, here, rows, up_hi, up_lo, recon_high.shape[2], strain_high.shape[0])
+    out = call_filter(here, strain, up_hi, up_lo, recon_high.shape[2], strain_high.shape[0])
     return out[None]
 
 

time: 68.8 us -> 62 us (0.901)
  blocking collectives: 28.6 us -> 53.1 us
  starting transfers between devices: 13.7 us -> 0 us
  waiting for transfers between devices: 10 us -> 0 us
  Pallas kernels: 12.9 us -> 8.72 us
  local copies, waits for them, and re-layouts: 1.97 us -> 0.01 us
  other arithmetic: 1.25 us -> 0 us
    all_to_all x0 -> x1, blocking collectives: none -> 24.8 us  [local(): got = lax.all_to_all(packed, 'tmpl', 0, 0, tiled=True)]
    all_to_all x1 -> x0, starting transfers between devices: 13.7 us -> none  [local(): got = lax.all_to_all(packed, 'tmpl', 0, 0, tiled=True)]
    all_to_all x1 -> x0, waiting for transfers between devices: 10 us -> none  [local(): got = lax.all_to_all(packed, 'tmpl', 0, 0, tiled=True)]
    pallas_call x3, Pallas kernels: 12.9 us -> 8.72 us  [the longest x1 6.69 us: call_filter(): pl.pallas_call(functools.partial(filter_and_rebuild, place), out_shape=ja...]
    slice x1 -> x0, local copies, waits for them, and re-layouts: 1.28 us -> none  [local(): rows[-8:]]
    concatenate x1 -> x0, other arithmetic: 1.25 us -> none  [local(): jnp.concatenate([jnp.stack([band, slot]), basis_count, jnp.zeros((3,), jn...]
  transfers between devices with their start and end apart: 1 -> 0, of which waited for: 1 -> 0; matrix products, arithmetic and copies ran while one was open for 2% -> 0% of each run, Pallas kernels for 0% -> 0%
where the time goes in v2:
time: 62 us; the launch traced here: 61.9 us
  blocking collectives  53.1 us (86%)
  Pallas kernels  8.72 us (14%)
    all_to_all x1, blocking collectives, local(): here = lax.all_to_all(sent, ('band', 'tm'), 0, 0, tiled=True)  28.3 us
    all_to_all x1, blocking collectives, local(): got = lax.all_to_all(packed, 'tmpl', 0, 0, tiled=True)  24.8 us
    pallas_call x1, Pallas kernels, call_filter(): pl.pallas_call(functools.partial(filter_and_rebuild, place), out_shape=ja...  6.69 us
    pallas_call x1, Pallas kernels, call_pack(): pl.pallas_call(functools.partial(pack_filters, place), out_shape=(pltpu.V...  1.51 us

profile of v2, /device:TPU:1, one launch (start us, length us, event | category | flops | bytes accessed | tf_op | source)
XLA Modules:
  0.0 61.9 jit_solution(9061585243004820861)
XLA Ops:
  0.0 0.0 copy-start
  0.0 0.0 copy-start.1
  0.0 1.5 %pack_filters.1 = (f32[32,16,128]{2,1,0:T(8,128)S(1)}, bf16[128,320]{1,0:T(8,128)(2,1)S(1)}, bf16[128,320]{1,0:T(8,128)(2,1)S(1)}, bf16[128,320]{1,0:T(8,128)(2,...) custom-call(s32[3]{0:T(128)} %count_ref.1, f32[10,1024]{1,0:T(8,128)} %high_ref.1, f32[10,1024]{1,0:T(8,128)} %mid_ref.1, ...), custom_call_target="tpu_custom_call" | custom-call | tf_op jit(solution)/shard_map/pack_filters/pallas_call | solution.py:290
  1.5 24.8 %all_to_all.10.got_ref = f32[32,16,128]{2,1,0:T(8,128)S(1)} all-to-all(f32[32,16,128]{2,1,0:T(8,128)S(1)} %get-tuple-element.11), channel_id=1, replica_groups=mesh['band'=2,'tmpl'=32,'tm'=8] {'tmpl'}, dimensions={0} | all-to-all | bytes 524288 | tf_op jit(solution)/shard_map/all_to_all | solution.py:361
  26.3 0.5 combine.1
  26.9 28.3 %all_to_all.11.got_ref = f32[16,80,128]{2,1,0:T(8,128)S(1)} all-to-all(f32[16,80,128]{2,1,0:T(8,128)S(1)} %combine.1), channel_id=1, replica_groups=mesh['band'=2,'tmpl'=32,'tm'=8] {'band','tm'}, dimensions={0} | all-to-all | bytes 1310720 | tf_op jit(solution)/shard_map/all_to_all | solution.py:363
  55.2 0.0 copy-done
  55.2 0.0 copy-done.1
  55.2 6.7 %filter_and_rebuild.1 = f32[64,8192]{1,0:T(8,128)} custom-call(f32[16,80,128]{2,1,0:T(8,128)S(1)} %all_to_all.11.got_ref, f32[80,128]{1,0:T(8,128)S(1)} %get-tuple-element.16.strain_ref, bf16[4,256,256]{2,1,0:T(8,128)(2,1)S(1)} %copy-done.1, bf16[4,256,256]{2,1,0:T(8,128)(2,1)S(1)} %copy-done), custom_call_target="tpu_custom_call" | custom-call | tf_op jit(solution)/shard_map/filter_and_rebuild/pallas_call | solution.py:312
Async XLA Ops:
  0.0 55.2 %copy-start = (bf16[4,256,256]{2,1,0:T(8,128)(2,1)S(1)}, bf16[4,256,256]{2,1,0:T(8,128)(2,1)}, u32[]{:S(2)}) copy-start(bf16[4,256,256]{2,1,0:T(8,128)(2,1)} %constant.9.up_lo_ref) | copy-start | bytes 1572868
  0.0 55.2 %copy-start.1 = (bf16[4,256,256]{2,1,0:T(8,128)(2,1)S(1)}, bf16[4,256,256]{2,1,0:T(8,128)(2,1)}, u32[]{:S(2)}) copy-start(bf16[4,256,256]{2,1,0:T(8,128)(2,1)} %constant.6.up_hi_ref) | copy-start | bytes 1572868
